TPU v7x, 32 devices: a whole 2x2x4 slice. The times are simulated.
32 devices in a mesh: emb: 8 (over z, x), seq: 4 (over y, core).
Axes of the slice: x: 2, y: 2, z: 4, core: 2. Of those that a mesh axis runs over, the one named last changes fastest.
Arguments:
- item_table: bfloat16 [32768, 512], P('emb'), may hold values from -6 to 6
- fetch_rows: int32 [8, 4, 8, 64], P('emb', 'seq'), may hold values from 0 to 4095
- event_slot: int32 [32768], P(('emb', 'seq')), may hold values from 0 to 511, as said below
- lengths: int32 [32, 8], P(('emb', 'seq')), may hold values from 1 to 512, 1024 in all within a row
- in_weight: bfloat16 [512, 2048], replicated, may hold values from -0.25 to 0.25
- out_weight: bfloat16 [512, 512], replicated, may hold values from -0.25 to 0.25
- out_grad: bfloat16 [32768, 512], P(('emb', 'seq')), may hold values from -6 to 6
Outputs:
- layer_out: bfloat16 [32768, 512], P(('emb', 'seq'))
- table_grad: float32 [32768, 512], P(('emb', 'seq'))
- in_weight_grad: float32 [512, 2048], replicated
- out_weight_grad: float32 [512, 512], replicated
Inputs may be any that keep to these rules, and one draw needn't show every extreme that they name: `event_slot`: within each buffer of 1024 events every slot 0 to 511 is named by at least one event.
All inputs are finite; a program needn't handle non-finite values.
Results may differ from a plain program's by a relative error of at most 0.02.
Values may be sent and summed in bfloat16 or wider, within the bound.
No kernel may reach another device: no remote copies, remote signals or barrier semaphores. Data moves between devices by JAX's collectives and lax.ppermute only.
A program may use at most 192 MiB of HBM per device.

v0:
```python
import jax
import jax.numpy as jnp
from jax import lax
from jax.sharding import PartitionSpec as P

HEADS = 4
MOST = 512
EPS = 1e-05


def normalize(rows_in):
    center = rows_in - jnp.mean(rows_in, axis=-1, keepdims=True)
    spread = jnp.mean(center * center, axis=-1, keepdims=True)
    return center * lax.rsqrt(spread + EPS)


def hstu_layer(events, in_weight, out_weight, lengths_row):
    rows_count, model_width = events.shape
    head_size = model_width // HEADS
    normed = normalize(events.astype(jnp.float32)).astype(jnp.bfloat16)
    hidden = jax.nn.silu(jnp.dot(normed, in_weight, preferred_element_type=jnp.float32))
    update_gate = hidden[:, :model_width]
    values = (
        hidden[:, model_width : 2 * model_width]
        .astype(jnp.bfloat16)
        .reshape(rows_count, HEADS, head_size)
    )
    queries = (
        hidden[:, 2 * model_width : 3 * model_width]
        .astype(jnp.bfloat16)
        .reshape(rows_count, HEADS, head_size)
    )
    key_rows = (
        hidden[:, 3 * model_width :].astype(jnp.bfloat16).reshape(rows_count, HEADS, head_size)
    )
    scores = jnp.einsum(
        "ihd,jhd->hij", queries, key_rows, preferred_element_type=jnp.float32
    ) * head_size ** (-0.5)
    places = jnp.arange(rows_count, dtype=jnp.int32)
    seq_ends = jnp.cumsum(lengths_row)
    segment = jnp.sum((places[:, None] >= seq_ends[None, :]).astype(jnp.int32), axis=1)
    allowed = (segment[:, None] == segment[None, :]) & (places[None, :] <= places[:, None])
    weights = jnp.where(allowed[None], jax.nn.silu(scores) / MOST, 0.0).astype(jnp.bfloat16)
    attended = jnp.einsum(
        "hij,jhd->ihd", weights, values, preferred_element_type=jnp.float32
    ).reshape(rows_count, model_width)
    gated_rows = (normalize(attended) * update_gate).astype(jnp.bfloat16)
    return (
        jnp.dot(gated_rows, out_weight, preferred_element_type=jnp.float32)
        + events.astype(jnp.float32)
    ).astype(jnp.bfloat16)


def on_device(item_table, fetch_rows, event_slot, lengths, in_weight, out_weight, out_grad):
    emb_count = lax.axis_size("emb")
    seq_count = lax.axis_size("seq")
    model_width = item_table.shape[1]
    shard_rows = item_table.shape[0]
    requests = fetch_rows.reshape(emb_count, -1)
    slot_count = requests.shape[0] * requests.shape[1]
    asked_rows = lax.all_to_all(requests, "emb", split_axis=0, concat_axis=0, tiled=True)
    found = item_table[asked_rows]
    fetched, asked_rows = (
        lax.all_to_all(found, "emb", split_axis=0, concat_axis=0, tiled=True),
        asked_rows,
    )
    slot_table = fetched.reshape(slot_count, model_width)
    events = slot_table[event_slot]
    lengths_row = lengths[0]

    def forward(rows_x, first, second):
        return hstu_layer(rows_x, first, second, lengths_row)

    layer_out, pullback = jax.vjp(forward, events, in_weight, out_weight)
    row_grad, first_grad, second_grad = pullback(out_grad)
    slot_grad = jax.ops.segment_sum(
        row_grad.astype(jnp.float32), event_slot, num_segments=slot_count
    )
    returned = lax.all_to_all(
        slot_grad.reshape(emb_count, -1, model_width).astype(jnp.bfloat16),
        "emb",
        split_axis=0,
        concat_axis=0,
        tiled=True,
    ).astype(jnp.float32)
    quarter = shard_rows // seq_count
    shared, shared_rows = (
        lax.all_gather(returned.astype(jnp.bfloat16), "seq", axis=0, tiled=True).astype(
            returned.dtype
        ),
        lax.all_gather(asked_rows, "seq", axis=0, tiled=True),
    )
    local_rows = shared_rows.reshape(-1) - lax.axis_index("seq") * quarter
    inside = (local_rows >= 0) & (local_rows < quarter)
    target = jnp.where(inside, local_rows, quarter)
    table_grad = jax.ops.segment_sum(
        shared.reshape(-1, model_width), target, num_segments=quarter + 1
    )[:quarter]
    in_total, out_total = lax.psum(
        (first_grad.astype(jnp.float32), second_grad.astype(jnp.float32)), ("emb", "seq")
    )
    return (layer_out, table_grad, in_total, out_total)


def solution(mesh):
    placed = (
        P("emb", None),
        P("emb", "seq", None, None),
        P(("emb", "seq")),
        P(("emb", "seq"), None),
        P(),
        P(),
        P(("emb", "seq"), None),
    )
    return jax.shard_map(
        on_device,
        mesh=mesh,
        in_specs=placed,
        out_specs=(P(("emb", "seq"), None), P(("emb", "seq"), None), P(), P()),
        check_vma=False,
    )
```

profile of v0, /device:TPU:0, one launch (start us, length us, event | category | flops | bytes accessed | tf_op | source)
XLA Modules:
  0.0 345.2 jit_solution(15317950688414619498)
XLA Ops:
  8.0 13.8 %all_to_all.25 = s32[8,1,64]{2,1,0:T(1,128)S(1)} all-to-all(s32[8,1,64]{2,1,0:T(1,128)} %bitcast.80), channel_id=1, replica_groups=mesh['emb'=8,'seq'=4] {'emb'}, dimensions={0} | all-to-all | bytes 4096 | tf_op jit(solution)/shard_map/all_to_all | solution.py:61
  22.0 5.4 %gather_fusion = bf16[512,512]{1,0:T(8,128)(2,1)} fusion(bf16[4096,512]{1,0:T(8,128)(2,1)} %param.7, s32[1024]{0:T(1024)S(1)} %pad_clamp_fusion), kind=kCustom, calls=%fused_computation | custom fusion | bytes 1050624 | tf_op jit(solution)/shard_map/gather | solution.py:62
  27.3 3.5 %all-to-all-start.1 = ((bf16[8,64,512]{2,1,0:T(8,128)(2,1)}), bf16[8,64,512]{2,1,0:T(8,128)(2,1)S(1)}, u32[]{:S(2)}, u32[]{:S(2)}) async-start(bf16[8,64,512]{2,1,0:T(8,128)(2,1)} %bitcast.2), calls=%async_computation.1 | async-start | bytes 1048576 | tf_op jit(solution)/shard_map/all_to_all | solution.py:64
  30.9 0.2 reduce-window.8
  31.1 0.1 convert_reduce_fusion.1
  31.2 1.6 fusion.8
  32.8 11.3 %all-to-all-done.1 = bf16[8,64,512]{2,1,0:T(8,128)(2,1)S(1)} async-done(((bf16[8,64,512]{2,1,0:T(8,128)(2,1)}), bf16[8,64,512]{2,1,0:T(8,128)(2,1)S(1)}, u32[]{:S(2)}, u32[]{:S(2)}) %all-to-all-start.1) | async-done | bytes 524320 | tf_op jit(solution)/shard_map/all_to_all | solution.py:64
  44.1 5.3 %gather_fusion.1 = bf16[1024,512]{1,0:T(8,128)(2,1)} fusion(bf16[512,512]{1,0:T(8,128)(2,1)S(1)} %bitcast.63, s32[1024]{0:T(1024)S(1)} %fusion.37), kind=kCustom, calls=%fused_computation.1 | custom fusion | bytes 2101248 | tf_op jit(solution)/shard_map/gather | solution.py:68
  49.4 1.4 convert_reduce_fusion
  50.9 1.7 fusion.14
  52.6 8.6 %fusion.44 = (bf16[1024,2048]{1,0:T(8,128)(2,1)S(1)}, f32[1024,2048]{1,0:T(8,128)}, f32[1024,2048]{1,0:T(8,128)}) fusion(bf16[512,2048]{1,0:T(8,128)(2,1)S(1)} %copy-done, bf16[1024,512]{1,0:T(8,128)(2,1)} %gather_fusion.1, f32[1024]{0:T(1024)S(1)} %fusion.38, f32[1024]{0:T(1024)S(1)} %broadcast_multiply_fusion.1), kind=kOutput, calls=%fused_computation.87 | convolution fusion | flops 2160066560 | bytes 24125440 | tf_op jit(solution)/shard_map/jvp()/dot_general | solution.py:21
  61.2 1.7 slice_bitcast_fusion
  62.9 2.3 copy.89
  65.2 1.3 copy.90
  66.5 11.8 %select_convert_fusion = (bf16[4,1024,1024]{2,1,0:T(8,128)(2,1)S(1)}, f32[4,1024,1024]{2,1,0:T(8,128)}) fusion(pred[1024,1024]{1,0:T(8,128)(4,1)} %fusion.8, bf16[1024,4,128]{0,2,1:T(8,128)(2,1)} %bitcast.72, bf16[1024,4,128]{0,2,1:T(8,128)(2,1)} %bitcast.74), kind=kOutput, calls=%fused_computation.8 | convolution fusion | flops 1107296256 | bytes 28311552 | tf_op jit(solution)/shard_map/jvp(ihd,jhd->hij)/dot_general | solution.py:36
  78.3 2.9 fusion.46
  81.2 0.3 copy-done.2
  81.5 1.3 copy-done.6
  82.8 0.3 fusion.19
  83.1 2.9 copy.84
  86.0 3.4 multiply_reduce_fusion
  89.4 3.6 %fusion.43 = (f32[1024]{0:T(1024)S(1)}, f32[1024,512]{1,0:T(8,128)S(1)}, bf16[1024,512]{1,0:T(8,128)(2,1)}, f32[1024,512]{1,0:T(8,128)}) fusion(f32[1024]{0:T(1024)S(1)} %get-tuple-element.15, f32[1024,512]{1,0:T(8,128)S(1)} %copy-done.5, f32[1024]{0:T(1024)S(1)} %broadcast_multiply_fusion, f32[1024]{0:T(1024)S(1)} %get-tuple-element.16, ...), kind=kLoop, calls=%fused_computation.86 | loop fusion | flops 6290432 | bytes 10502144 | tf_op jit(solution)/shard_map/transpose(jvp())/reduce_sum | solution.py:12
  93.1 1.2 broadcast_add_fusion
  94.3 1.5 copy.85
  95.8 15.3 %fusion.2 = bf16[4,1024,1024]{2,1,0:T(8,128)(2,1)} fusion(f32[4,1024,1024]{2,1,0:T(8,128)} %get-tuple-element.19, pred[1024,1024]{1,0:T(8,128)(4,1)} %fusion.8, bf16[4,128,1024]{2,1,0:T(8,128)(2,1)S(1)} %bitcast.67, bf16[128,4,8,128]{3,2,1,0:T(8,128)(2,1)} %get-tuple-element.11), kind=kOutput, calls=%fused_computation.7 | convolution fusion | flops 1136656384 | bytes 28311552 | tf_op jit(solution)/shard_map/transpose(jvp(hij,jhd->ihd))/dot_general | solution.py:44
  111.0 5.8 %fusion.49 = bf16[4,1024,128]{1,2,0:T(8,128)(2,1)} fusion(bf16[4,1024,1024]{2,1,0:T(8,128)(2,1)} %fusion.2, bf16[1024,4,128]{0,2,1:T(8,128)(2,1)S(1)} %bitcast.73), kind=kOutput, calls=%fused_computation.91 | convolution fusion | flops 1073741824 | bytes 10485760 | tf_op jit(solution)/shard_map/transpose(jvp(ihd,jhd->hij))/dot_general | solution.py:36
  116.9 7.5 %fusion.48 = bf16[4,1024,128]{1,2,0:T(8,128)(2,1)} fusion(bf16[4,1024,1024]{2,1,0:T(8,128)(2,1)} %fusion.2, bf16[1024,4,128]{0,2,1:T(8,128)(2,1)S(1)} %bitcast.75), kind=kOutput, calls=%fused_computation.90 | convolution fusion | flops 1073741824 | bytes 10485760 | tf_op jit(solution)/shard_map/transpose(jvp(ihd,jhd->hij))/dot_general | solution.py:36
  124.4 2.3 fusion.47
  126.7 2.4 copy.86
  129.1 2.3 copy.87
  131.4 1.3 copy.88
  132.7 7.1 %fusion.4 = bf16[1024,2048]{1,0:T(8,128)(2,1)S(1)} fusion(f32[1024,2048]{1,0:T(8,128)} %get-tuple-element.17, f32[1024,512]{1,0:T(8,128)} %get-tuple-element.14, bf16[1024,512]{1,0:T(8,128)(2,1)} %copy.88, bf16[1024,512]{1,0:T(8,128)(2,1)} %copy.87, bf16[1024,512]{1,0:T(8,128)(2,1)} %copy.86), kind=kLoop, calls=%fused_computation.12 | loop fusion | flops 33554432 | bytes 17825792 | tf_op jit(solution)/shard_map/transpose(jvp(jit(silu)))/add_any | solution.py:21
  139.8 2.5 fusion.16
  142.3 0.9 copy-done.7
  143.3 1.0 fusion.22
  144.3 9.1 %scatter_custom_fusion = f32[512,512]{1,0:T(8,128)} fusion(s32[1024]{0:T(1024)S(1)} %copy-done.14, bf16[1024,512]{1,0:T(8,128)(2,1)} %param.13, bf16[1024,512]{1,0:T(8,128)(2,1)S(1)} %copy-done.1, bf16[1024,512]{1,0:T(8,128)(2,1)} %copy-done.7, f32[1024]{0:T(1024)S(1)} %negate_multiply_fusion, f32[1024]{0:T(1024)S(1)} %multiply_multiply_fusion, ...), kind=kCustom, calls=%fused_computation.40 | custom fusion | flops 6291456 | bytes 4210692 | tf_op jit(solution)/shard_map/scatter-add | solution.py:76
  153.4 1.3 convert_element_type.125
  154.7 17.4 %all_to_all.26 = bf16[8,64,512]{2,1,0:T(8,128)(2,1)} all-to-all(bf16[8,64,512]{2,1,0:T(8,128)(2,1)S(1)} %bitcast.70), channel_id=1, replica_groups=mesh['emb'=8,'seq'=4] {'emb'}, dimensions={0} | all-to-all | bytes 1048576 | tf_op jit(solution)/shard_map/all_to_all | solution.py:79
  172.1 3.4 fusion.23
  175.5 4.6 %fusion.13 = f32[512,2048]{1,0:T(8,128)} fusion(bf16[1024,2048]{1,0:T(8,128)(2,1)S(1)} %copy-done.4, bf16[1024,512]{1,0:T(8,128)(2,1)S(1)} %copy-done.1, f32[1024]{0:T(1024)S(1)} %fusion.38, f32[1024]{0:T(1024)S(1)} %broadcast_multiply_fusion.1), kind=kOutput, calls=%fused_computation.29 | convolution fusion | flops 2150629376 | bytes 9445376 | tf_op jit(solution)/shard_map/transpose(jvp())/dot_general | solution.py:21
  180.2 5.4 %all-gather = s32[32,1,64]{2,1,0:T(1,128)S(1)} all-gather(s32[8,1,64]{2,1,0:T(1,128)S(1)} %all_to_all.25), channel_id=2, replica_groups=mesh['emb'=8,'seq'=4] {'seq'}, dimensions={0}, use_global_device_ids=true | all-gather | bytes 10240 | tf_op jit(solution)/shard_map/all_gather | solution.py:91
  185.7 3.1 fusion.17
  188.8 5.5 %all-gather.3.cloned.1.call-done = bf16[32,64,512]{2,1,0:T(8,128)(2,1)} async-done(((bf16[8,64,512]{2,1,0:T(8,128)(2,1)}), bf16[32,64,512]{2,1,0:T(8,128)(2,1)}) %all-gather.3.cloned.1.call-update) | async-done | bytes 2097168 | tf_op jit(solution)/shard_map/all_gather | solution.py:88
  194.3 15.0 %scatter_custom_fusion.1 = f32[1025,512]{1,0:T(8,128)} fusion(s32[2048]{0:T(1024)S(1)} %bitcast.79, bf16[2048,512]{1,0:T(8,128)(2,1)} %bitcast.71, f32[]{:T(128)} %constant.22.clone.1), kind=kCustom, calls=%fused_computation.15 | custom fusion | flops 2097152 | bytes 4196356 | tf_op jit(solution)/shard_map/scatter-add | solution.py:96
  209.3 3.1 slice.31
  212.4 119.4 %all-reduce.7.cloned.1.call-done = (f32[512,2048]{1,0:T(8,128)}, f32[512,512]{1,0:T(8,128)}) async-done(((f32[512,2048]{1,0:T(8,128)}, f32[512,512]{1,0:T(8,128)}), (f32[512,2048]{1,0:T(8,128)}, f32[512,512]{1,0:T(8,128)})) %all-reduce.7.cloned.1.call-update) | async-done | bytes 5242896 | tf_op jit(solution)/shard_map/psum | solution.py:99
  331.8 4.8 %copy.104 = f32[512,2048]{1,0:T(8,128)} copy(f32[512,2048]{1,0:T(8,128)} %get-tuple-element.28) | data formatting | bytes 8388608
  336.6 1.0 copy.105
  (52 shorter events, 0.5 us)
Async XLA Ops:
  8.0 44.6 %copy-start = (bf16[512,2048]{1,0:T(8,128)(2,1)S(1)}, bf16[512,2048]{1,0:T(8,128)(2,1)}, u32[]{:S(2)}) copy-start(bf16[512,2048]{1,0:T(8,128)(2,1)} %param.11) | copy-start | bytes 6291460
  8.0 22.9 %copy-start.15 = (s32[1,8]{1,0:T(1,128)S(1)}, s32[1,8]{1,0:T(1,128)}, u32[]{:S(2)}) copy-start(s32[1,8]{1,0:T(1,128)} %param.10) | copy-start | bytes 100
  8.0 23.2 %copy-start.14 = (s32[1024]{0:T(1024)S(1)}, s32[1024]{0:T(1024)}, u32[]{:S(2)}) copy-start(s32[1024]{0:T(1024)} %param.9) | copy-start | bytes 12292
  27.3 16.8 %all-to-all-start.1 = ((bf16[8,64,512]{2,1,0:T(8,128)(2,1)}), bf16[8,64,512]{2,1,0:T(8,128)(2,1)S(1)}, u32[]{:S(2)}, u32[]{:S(2)}) async-start(bf16[8,64,512]{2,1,0:T(8,128)(2,1)} %bitcast.2), calls=%async_computation.1 | async-start | bytes 1048576 | tf_op jit(solution)/shard_map/all_to_all | solution.py:64
  30.8 163.4 %all-gather.3.cloned.1.call-start = ((), (), s32[]{:S(2)}) async-start(), calls=%async_computation.3 | async-start | bytes 2621440 | tf_op jit(solution)/shard_map/all_gather | solution.py:88
  66.5 11.8 %copy-start.10 = (bf16[128,4,8,128]{3,2,1,0:T(8,128)(2,1)S(1)}, bf16[128,4,8,128]{3,2,1,0:T(8,128)(2,1)}, u32[]{:S(2)}) copy-start(bf16[128,4,8,128]{3,2,1,0:T(8,128)(2,1)} %get-tuple-element.11) | copy-start | bytes 3145732
  78.3 3.2 copy-start.2
  81.5 1.3 copy-start.6
  81.5 4.5 %copy-start.9 = (bf16[1024,512]{1,0:T(8,128)(2,1)S(1)}, bf16[1024,512]{1,0:T(8,128)(2,1)}, u32[]{:S(2)}) copy-start(bf16[1024,512]{1,0:T(8,128)(2,1)} %param.13) | copy-start | bytes 3145732
  86.0 3.4 copy-start.5
  95.8 15.3 %copy-start.11 = (bf16[1024,512]{0,1:T(8,128)(2,1)S(1)}, bf16[1024,512]{0,1:T(8,128)(2,1)}, u32[]{:S(2)}) copy-start(bf16[1024,512]{0,1:T(8,128)(2,1)} %copy.89) | copy-start | bytes 3145732
  111.0 5.8 %copy-start.12 = (bf16[1024,512]{0,1:T(8,128)(2,1)S(1)}, bf16[1024,512]{0,1:T(8,128)(2,1)}, u32[]{:S(2)}) copy-start(bf16[1024,512]{0,1:T(8,128)(2,1)} %copy.90) | copy-start | bytes 3145732
  111.0 13.3 %slice-start = ((s8[8388608]{0:T(1024)(128)(4,1)}), s8[4194304]{0:T(1024)(128)(4,1)S(1)}, s32[]{:S(2)}) async-start(s8[8388608]{0:T(1024)(128)(4,1)} %bitcast.64), calls=%async_computation.5 | async-start | bytes 8388608
  116.9 7.5 %slice-start.1 = ((s8[8388608]{0:T(1024)(128)(4,1)}), s8[4194304]{0:T(1024)(128)(4,1)S(1)}, s32[]{:S(2)}) async-start(s8[8388608]{0:T(1024)(128)(4,1)} %bitcast.64), calls=%async_computation.6 | async-start | bytes 8388608
  126.7 4.7 %copy-start.8 = (bf16[4,128,1024]{2,1,0:T(8,128)(2,1)S(1)}, bf16[4,128,1024]{2,1,0:T(8,128)(2,1)}, u32[]{:S(2)}) copy-start(bf16[4,128,1024]{2,1,0:T(8,128)(2,1)} %fusion.47) | copy-start | bytes 3145732
  132.7 7.1 %copy-start.1 = (bf16[1024,512]{1,0:T(8,128)(2,1)S(1)}, bf16[1024,512]{1,0:T(8,128)(2,1)}, u32[]{:S(2)}) copy-start(bf16[1024,512]{1,0:T(8,128)(2,1)} %gather_fusion.1) | copy-start | bytes 3145732
  139.8 2.5 copy-start.3
  142.3 1.0 copy-start.7
  172.1 159.7 %all-reduce.7.cloned.1.call-start = ((), (), s32[]{:S(2)}) async-start(), calls=%async_computation.4 | async-start | bytes 10485760 | tf_op jit(solution)/shard_map/psum | solution.py:99
  172.1 3.4 copy-start.4
  331.8 4.8 %copy-start.13 = (f32[512,512]{1,0:T(8,128)S(1)}, f32[512,512]{1,0:T(8,128)}, u32[]{:S(2)}) copy-start(f32[512,512]{1,0:T(8,128)} %get-tuple-element.29) | copy-start | bytes 3145732
Sparse Core Ops, SparseCore 0:
  172.2 22.0 all-gather.2
Sparse Core Ops, SparseCore 1:
  180.3 151.5 all-reduce.6
where the time goes:
time: 348 us; the launch traced here: 345 us
  waiting for transfers between devices  136 us (39%)
  matrix products  71.2 us (20%)
  other arithmetic  43.7 us (13%)
  local copies, waits for them, and re-layouts  38 us (11%)
  blocking collectives  36.6 us (11%)
  between operations  15.9 us (5%)
  starting transfers between devices  3.58 us (1%)
    psum x1, waiting for transfers between devices, on_device(): lax.psum((first_grad.astype(jnp.float32), second_grad.astype(jnp.float32)...  119 us
    dot_general x3, matrix products, hstu_layer(): jnp.einsum('ihd,jhd->hij', queries, key_rows, preferred_element_type=jnp....  25.1 us
    dot_general x3, matrix products, hstu_layer(): jnp.einsum('hij,jhd->ihd', weights, values, preferred_element_type=jnp.fl...  20.5 us
    all_to_all x1, blocking collectives, on_device(): lax.all_to_all(slot_grad.reshape(emb_count, -1, model_width).astype(jnp.b...  17.4 us
    dot_general x3, matrix products, hstu_layer(): jnp.dot(normed, in_weight, preferred_element_type=jnp.float32)  15.7 us
    scatter-add x1, other arithmetic, on_device(): jax.ops.segment_sum(shared.reshape(-1, model_width), target, num_segments...  15 us
    all_to_all x1, blocking collectives, on_device(): lax.all_to_all(requests, 'emb', split_axis=0, concat_axis=0, tiled=True)  13.8 us
    all_to_all x1, waiting for transfers between devices, on_device(): lax.all_to_all(found, 'emb', split_axis=0, concat_axis=0, tiled=True)  11.3 us
  transfers between devices with their start and end apart: 3, of which 3 were waited for; matrix products, arithmetic and copies ran while one was open for 9% of the time, Pallas kernels for 0%

commit v1 on v0

--- a/solution.py
+++ b/solution.py
@@ -6,6 +6,11 @@
 HEADS = 4
 MOST = 512
 EPS = 1e-05
+
+
+def one_after_other(x, axis_one, axis_two):
+    partial = lax.psum(x, axis_one)
+    return lax.psum(partial, axis_two)
 
 
 def normalize(rows_in):
@@ -96,8 +101,8 @@
     table_grad = jax.ops.segment_sum(
         shared.reshape(-1, model_width), target, num_segments=quarter + 1
     )[:quarter]
-    in_total, out_total = lax.psum(
-        (first_grad.astype(jnp.float32), second_grad.astype(jnp.float32)), ("emb", "seq")
+    in_total, out_total = one_after_other(
+        (first_grad.astype(jnp.float32), second_grad.astype(jnp.float32)), "seq", "emb"
     )
     return (layer_out, table_grad, in_total, out_total)
 

time: 348 us -> 474 us (1.36)
  waiting for transfers between devices: 136 us -> 264 us
    psum x1 -> x2, waiting for transfers between devices: 119 us -> 237 us  [the longest x1 170 us: one_after_other(): return lax.psum(partial, axis_two)]
    all_gather x1, waiting for transfers between devices: 5.5 us -> 15.9 us  [on_device(): lax.all_gather(returned.astype(jnp.bfloat16), 'seq', axis=0, tiled=True)]
    unnamed x39 -> x41, local copies, waits for them, and re-layouts: 10.1 us -> 10.1 us
  transfers between devices with their start and end apart: 3 -> 4, of which waited for: 3 -> 4; matrix products, arithmetic and copies ran while one was open for 9% -> 8% of each run, Pallas kernels for 0% -> 0%
where the time goes in v1:
time: 474 us; the launch traced here: 471 us
  waiting for transfers between devices  264 us (56%)
  matrix products  71.3 us (15%)
  other arithmetic  43.3 us (9%)
  local copies, waits for them, and re-layouts  38.1 us (8%)
  blocking collectives  36.7 us (8%)
  between operations  14.2 us (3%)
    psum x1, waiting for transfers between devices, one_after_other(): return lax.psum(partial, axis_two)  170 us
    psum x1, waiting for transfers between devices, one_after_other(): partial = lax.psum(x, axis_one)  66.8 us
    dot_general x3, matrix products, hstu_layer(): jnp.einsum('ihd,jhd->hij', queries, key_rows, preferred_element_type=jnp....  25.1 us
    dot_general x3, matrix products, hstu_layer(): jnp.einsum('hij,jhd->ihd', weights, values, preferred_element_type=jnp.fl...  20.2 us
    dot_general x3, matrix products, hstu_layer(): jnp.dot(normed, in_weight, preferred_element_type=jnp.float32)  17.8 us
    all_to_all x1, blocking collectives, on_device(): lax.all_to_all(slot_grad.reshape(emb_count, -1, model_width).astype(jnp.b...  17.6 us
    all_gather x1, waiting for transfers between devices, on_device(): lax.all_gather(returned.astype(jnp.bfloat16), 'seq', axis=0, tiled=True)  15.9 us
    scatter-add x1, other arithmetic, on_device(): jax.ops.segment_sum(shared.reshape(-1, model_width), target, num_segments...  14.8 us
  transfers between devices with their start and end apart: 4, of which 4 were waited for; matrix products, arithmetic and copies ran while one was open for 8% of the time, Pallas kernels for 0%

profile of v1, /device:TPU:0, one launch (start us, length us, event | category | flops | bytes accessed | tf_op | source)
XLA Modules:
  0.0 471.2 jit_solution(5368366663374485112)
XLA Ops:
  7.2 13.8 %all_to_all.25 = s32[8,1,64]{2,1,0:T(1,128)S(1)} all-to-all(s32[8,1,64]{2,1,0:T(1,128)} %bitcast.80), channel_id=1, replica_groups=mesh['emb'=8,'seq'=4] {'emb'}, dimensions={0} | all-to-all | bytes 4096 | tf_op jit(solution)/shard_map/all_to_all | solution.py:66
  21.1 5.4 %gather_fusion = bf16[512,512]{1,0:T(8,128)(2,1)} fusion(bf16[4096,512]{1,0:T(8,128)(2,1)} %param.7, s32[1024]{0:T(1024)S(1)} %pad_clamp_fusion), kind=kCustom, calls=%fused_computation | custom fusion | bytes 1050624 | tf_op jit(solution)/shard_map/gather | solution.py:67
  26.5 3.5 all-to-all-start.1
  30.4 1.6 fusion.8
  31.9 11.3 %all-to-all-done.1 = bf16[8,64,512]{2,1,0:T(8,128)(2,1)S(1)} async-done(((bf16[8,64,512]{2,1,0:T(8,128)(2,1)}), bf16[8,64,512]{2,1,0:T(8,128)(2,1)S(1)}, u32[]{:S(2)}, u32[]{:S(2)}) %all-to-all-start.1) | async-done | bytes 524320 | tf_op jit(solution)/shard_map/all_to_all | solution.py:69
  43.3 5.5 %gather_fusion.1 = bf16[1024,512]{1,0:T(8,128)(2,1)} fusion(bf16[512,512]{1,0:T(8,128)(2,1)S(1)} %bitcast.63, s32[1024]{0:T(1024)S(1)} %fusion.37), kind=kCustom, calls=%fused_computation.1 | custom fusion | bytes 2101248 | tf_op jit(solution)/shard_map/gather | solution.py:73
  48.8 1.4 convert_reduce_fusion
  50.2 1.7 fusion.14
  52.0 8.6 %fusion.44 = (bf16[1024,2048]{1,0:T(8,128)(2,1)S(1)}, f32[1024,2048]{1,0:T(8,128)}, f32[1024,2048]{1,0:T(8,128)}) fusion(bf16[512,2048]{1,0:T(8,128)(2,1)S(1)} %copy-done, bf16[1024,512]{1,0:T(8,128)(2,1)} %gather_fusion.1, f32[1024]{0:T(1024)S(1)} %fusion.38, f32[1024]{0:T(1024)S(1)} %broadcast_multiply_fusion.1), kind=kOutput, calls=%fused_computation.87 | convolution fusion | flops 2160066560 | bytes 24125440 | tf_op jit(solution)/shard_map/jvp()/dot_general | solution.py:26
  60.6 1.7 slice_bitcast_fusion
  62.3 2.3 copy.89
  64.5 1.3 copy.90
  65.9 11.8 %select_convert_fusion = (bf16[4,1024,1024]{2,1,0:T(8,128)(2,1)S(1)}, f32[4,1024,1024]{2,1,0:T(8,128)}) fusion(pred[1024,1024]{1,0:T(8,128)(4,1)} %fusion.8, bf16[1024,4,128]{0,2,1:T(8,128)(2,1)} %bitcast.72, bf16[1024,4,128]{0,2,1:T(8,128)(2,1)} %bitcast.74), kind=kOutput, calls=%fused_computation.8 | convolution fusion | flops 1107296256 | bytes 28311552 | tf_op jit(solution)/shard_map/jvp(ihd,jhd->hij)/dot_general | solution.py:41
  77.6 2.9 fusion.46
  80.6 0.3 copy-done.2
  80.8 1.3 copy-done.5
  82.2 0.3 fusion.19
  82.5 2.9 copy.84
  85.3 3.4 multiply_reduce_fusion
  88.8 3.6 fusion.43
  92.4 1.2 broadcast_add_fusion
  93.6 1.5 copy.85
  95.1 15.0 %fusion.2 = bf16[4,1024,1024]{2,1,0:T(8,128)(2,1)} fusion(f32[4,1024,1024]{2,1,0:T(8,128)} %get-tuple-element.21, pred[1024,1024]{1,0:T(8,128)(4,1)} %fusion.8, bf16[4,128,1024]{2,1,0:T(8,128)(2,1)S(1)} %bitcast.67, bf16[128,4,8,128]{3,2,1,0:T(8,128)(2,1)} %get-tuple-element.13), kind=kOutput, calls=%fused_computation.7 | convolution fusion | flops 1136656384 | bytes 28311552 | tf_op jit(solution)/shard_map/transpose(jvp(hij,jhd->ihd))/dot_general | solution.py:49
  110.1 5.8 %fusion.49 = bf16[4,1024,128]{1,2,0:T(8,128)(2,1)} fusion(bf16[4,1024,1024]{2,1,0:T(8,128)(2,1)} %fusion.2, bf16[1024,4,128]{0,2,1:T(8,128)(2,1)S(1)} %bitcast.73), kind=kOutput, calls=%fused_computation.91 | convolution fusion | flops 1073741824 | bytes 10485760 | tf_op jit(solution)/shard_map/transpose(jvp(ihd,jhd->hij))/dot_general | solution.py:41
  116.0 7.5 %fusion.48 = bf16[4,1024,128]{1,2,0:T(8,128)(2,1)} fusion(bf16[4,1024,1024]{2,1,0:T(8,128)(2,1)} %fusion.2, bf16[1024,4,128]{0,2,1:T(8,128)(2,1)S(1)} %bitcast.75), kind=kOutput, calls=%fused_computation.90 | convolution fusion | flops 1073741824 | bytes 10485760 | tf_op jit(solution)/shard_map/transpose(jvp(ihd,jhd->hij))/dot_general | solution.py:41
  123.5 2.3 fusion.47
  125.8 2.4 copy.86
  128.2 2.3 copy.87
  130.5 1.3 copy.88
  131.8 7.0 %fusion.4 = bf16[1024,2048]{1,0:T(8,128)(2,1)S(1)} fusion(f32[1024,2048]{1,0:T(8,128)} %get-tuple-element.19, f32[1024,512]{1,0:T(8,128)} %get-tuple-element.16, bf16[1024,512]{1,0:T(8,128)(2,1)} %copy.88, bf16[1024,512]{1,0:T(8,128)(2,1)} %copy.87, bf16[1024,512]{1,0:T(8,128)(2,1)} %copy.86), kind=kLoop, calls=%fused_computation.12 | loop fusion | flops 33554432 | bytes 17825792 | tf_op jit(solution)/shard_map/transpose(jvp(jit(silu)))/add_any | solution.py:26
  138.8 4.5 fusion.13
  143.3 1.7 fusion.23
  145.0 0.3 all-gather.3.cloned.1.call-start
  145.3 4.6 fusion.16
  149.9 0.9 copy-done.6
  150.9 1.0 fusion.22
  151.9 9.1 %scatter_custom_fusion = f32[512,512]{1,0:T(8,128)} fusion(s32[1024]{0:T(1024)S(1)} %copy-done.15, bf16[1024,512]{1,0:T(8,128)(2,1)} %param.13, bf16[1024,512]{1,0:T(8,128)(2,1)S(1)} %copy-done.1, bf16[1024,512]{1,0:T(8,128)(2,1)} %copy-done.6, f32[1024]{0:T(1024)S(1)} %negate_multiply_fusion, f32[1024]{0:T(1024)S(1)} %multiply_multiply_fusion, ...), kind=kCustom, calls=%fused_computation.40 | custom fusion | flops 6291456 | bytes 4210692 | tf_op jit(solution)/shard_map/scatter-add | solution.py:81
  161.0 1.3 convert_element_type.125
  162.3 17.6 %all_to_all.26 = bf16[8,64,512]{2,1,0:T(8,128)(2,1)} all-to-all(bf16[8,64,512]{2,1,0:T(8,128)(2,1)S(1)} %bitcast.70), channel_id=1, replica_groups=mesh['emb'=8,'seq'=4] {'emb'}, dimensions={0} | all-to-all | bytes 1048576 | tf_op jit(solution)/shard_map/all_to_all | solution.py:84
  180.0 66.8 %all-reduce.11.cloned.1.call-done = (f32[512,2048]{1,0:T(8,128)}, f32[512,512]{1,0:T(8,128)}) async-done(((f32[512,2048]{1,0:T(8,128)}, f32[512,512]{1,0:T(8,128)}), (f32[512,2048]{1,0:T(8,128)}, f32[512,512]{1,0:T(8,128)})) %all-reduce.11.cloned.1.call-update) | async-done | bytes 5242896 | tf_op jit(solution)/shard_map/psum | solution.py:12
  246.9 5.2 %all-gather = s32[32,1,64]{2,1,0:T(1,128)S(1)} all-gather(s32[8,1,64]{2,1,0:T(1,128)S(1)} %all_to_all.25), channel_id=2, replica_groups=mesh['emb'=8,'seq'=4] {'seq'}, dimensions={0}, use_global_device_ids=true | all-gather | bytes 10240 | tf_op jit(solution)/shard_map/all_gather | solution.py:96
  252.2 3.0 fusion.17
  255.2 15.9 %all-gather.3.cloned.1.call-done = bf16[32,64,512]{2,1,0:T(8,128)(2,1)} async-done(((bf16[8,64,512]{2,1,0:T(8,128)(2,1)}), bf16[32,64,512]{2,1,0:T(8,128)(2,1)}) %all-gather.3.cloned.1.call-update) | async-done | bytes 2097168 | tf_op jit(solution)/shard_map/all_gather | solution.py:93
  271.1 14.8 %scatter_custom_fusion.1 = f32[1025,512]{1,0:T(8,128)} fusion(s32[2048]{0:T(1024)S(1)} %bitcast.79, bf16[2048,512]{1,0:T(8,128)(2,1)} %bitcast.71, f32[]{:T(128)} %constant.22.clone.1), kind=kCustom, calls=%fused_computation.15 | custom fusion | flops 2097152 | bytes 4196356 | tf_op jit(solution)/shard_map/scatter-add | solution.py:101
  285.9 3.1 slice.31
  289.0 169.7 %all-reduce.9.cloned.1.call-done = (f32[512,2048]{1,0:T(8,128)}, f32[512,512]{1,0:T(8,128)}) async-done(((f32[512,2048]{1,0:T(8,128)}, f32[512,512]{1,0:T(8,128)}), (f32[512,2048]{1,0:T(8,128)}, f32[512,512]{1,0:T(8,128)})) %all-reduce.9.cloned.1.call-update) | async-done | bytes 5242896 | tf_op jit(solution)/shard_map/psum | solution.py:13
  458.7 4.8 %copy.106 = f32[512,2048]{1,0:T(8,128)} copy(f32[512,2048]{1,0:T(8,128)} %get-tuple-element.30) | data formatting | bytes 8388608
  463.5 1.0 copy.107
  (57 shorter events, 0.8 us)
Async XLA Ops:
  7.2 44.8 %copy-start = (bf16[512,2048]{1,0:T(8,128)(2,1)S(1)}, bf16[512,2048]{1,0:T(8,128)(2,1)}, u32[]{:S(2)}) copy-start(bf16[512,2048]{1,0:T(8,128)(2,1)} %param.11) | copy-start | bytes 6291460
  7.2 22.9 %copy-start.16 = (s32[1,8]{1,0:T(1,128)S(1)}, s32[1,8]{1,0:T(1,128)}, u32[]{:S(2)}) copy-start(s32[1,8]{1,0:T(1,128)} %param.10) | copy-start | bytes 100
  7.2 23.2 %copy-start.15 = (s32[1024]{0:T(1024)S(1)}, s32[1024]{0:T(1024)}, u32[]{:S(2)}) copy-start(s32[1024]{0:T(1024)} %param.9) | copy-start | bytes 12292
  26.5 16.8 %all-to-all-start.1 = ((bf16[8,64,512]{2,1,0:T(8,128)(2,1)}), bf16[8,64,512]{2,1,0:T(8,128)(2,1)S(1)}, u32[]{:S(2)}, u32[]{:S(2)}) async-start(bf16[8,64,512]{2,1,0:T(8,128)(2,1)} %bitcast.2), calls=%async_computation.1 | async-start | bytes 1048576 | tf_op jit(solution)/shard_map/all_to_all | solution.py:69
  30.0 216.8 %all-reduce.11.cloned.1.call-start = ((), (), s32[]{:S(2)}) async-start(), calls=%async_computation.5 | async-start | bytes 10485760 | tf_op jit(solution)/shard_map/psum | solution.py:12
  65.9 11.8 %copy-start.10 = (bf16[128,4,8,128]{3,2,1,0:T(8,128)(2,1)S(1)}, bf16[128,4,8,128]{3,2,1,0:T(8,128)(2,1)}, u32[]{:S(2)}) copy-start(bf16[128,4,8,128]{3,2,1,0:T(8,128)(2,1)} %get-tuple-element.13) | copy-start | bytes 3145732
  77.6 3.2 copy-start.2
  80.8 1.3 copy-start.5
  80.8 4.5 copy-start.8
  85.3 3.4 copy-start.4
  95.1 15.0 %copy-start.12 = (bf16[1024,512]{0,1:T(8,128)(2,1)S(1)}, bf16[1024,512]{0,1:T(8,128)(2,1)}, u32[]{:S(2)}) copy-start(bf16[1024,512]{0,1:T(8,128)(2,1)} %copy.89) | copy-start | bytes 3145732
  110.1 5.8 %copy-start.13 = (bf16[1024,512]{0,1:T(8,128)(2,1)S(1)}, bf16[1024,512]{0,1:T(8,128)(2,1)}, u32[]{:S(2)}) copy-start(bf16[1024,512]{0,1:T(8,128)(2,1)} %copy.90) | copy-start | bytes 3145732
  110.1 13.3 %slice-start = ((s8[8388608]{0:T(1024)(128)(4,1)}), s8[4194304]{0:T(1024)(128)(4,1)S(1)}, s32[]{:S(2)}) async-start(s8[8388608]{0:T(1024)(128)(4,1)} %bitcast.64), calls=%async_computation.6 | async-start | bytes 8388608
  116.0 7.5 %slice-start.1 = ((s8[8388608]{0:T(1024)(128)(4,1)}), s8[4194304]{0:T(1024)(128)(4,1)S(1)}, s32[]{:S(2)}) async-start(s8[8388608]{0:T(1024)(128)(4,1)} %bitcast.64), calls=%async_computation.7 | async-start | bytes 8388608
  125.8 4.7 copy-start.7
  131.8 7.0 %copy-start.1 = (bf16[1024,512]{1,0:T(8,128)(2,1)S(1)}, bf16[1024,512]{1,0:T(8,128)(2,1)}, u32[]{:S(2)}) copy-start(bf16[1024,512]{1,0:T(8,128)(2,1)} %gather_fusion.1) | copy-start | bytes 3145732
  138.8 4.5 copy-start.3
  138.8 4.5 copy-start.9
  138.8 4.5 copy-start.11
  145.0 126.1 %all-gather.3.cloned.1.call-start = ((), (), s32[]{:S(2)}) async-start(), calls=%async_computation.3 | async-start | bytes 2621440 | tf_op jit(solution)/shard_map/all_gather | solution.py:93
  149.9 1.0 copy-start.6
  180.0 278.7 %all-reduce.9.cloned.1.call-start = ((), (), s32[]{:S(2)}) async-start(), calls=%async_computation.4 | async-start | bytes 10485760 | tf_op jit(solution)/shard_map/psum | solution.py:13
  458.7 4.8 %copy-start.14 = (f32[512,512]{1,0:T(8,128)S(1)}, f32[512,512]{1,0:T(8,128)}, u32[]{:S(2)}) copy-start(f32[512,512]{1,0:T(8,128)} %get-tuple-element.31) | copy-start | bytes 3145732
Sparse Core Ops, SparseCore 0:
  145.1 101.6 all-reduce.10
  248.4 22.7 all-gather.2
  274.9 183.8 all-reduce.8
